TPU v7x, 32 devices: a whole 2x2x4 slice. The times are simulated.
32 devices in a mesh: grp: 4 (over z), ep: 8 (over y, x, core).
Axes of the slice: x: 2, y: 2, z: 4, core: 2. Of those that a mesh axis runs over, the one named last changes fastest.
Arguments:
- hidden: bfloat16 [4, 8, 32, 1024], P('grp', 'ep'), may hold values from -6 to 6
- down_weight: bfloat16 [8, 1024, 4096], P('ep'), may hold values from -0.1875 to 0.1875
- slot_gate: float32 [4, 8, 32], P('grp', 'ep'), may hold values from 0.02 to 0.6
- slot_owner: int32 [4, 8, 32], P('grp', 'ep'), may hold values from 0 to 3
- slot_row: int32 [4, 8, 32], P('grp', 'ep'), may hold values from 0 to 31
- block_count: int32 [4, 8, 8], P('grp', 'ep'), may hold values from 0 to 4, as said below
Outputs:
- mixed: bfloat16 [1024, 4096], P(('grp', 'ep'))
Inputs may be any that keep to these rules, and one draw needn't show every extreme that they name: `block_count`: every device's expert has at least one block with all 4 slots live.
All inputs are finite; a program needn't handle non-finite values.
Results may differ from a plain program's by a relative error of at most 0.009.
Values may be sent and summed in bfloat16 or wider, within the bound.
A program may use at most 64 MiB of HBM per device.

v0:
```python
import functools

import jax
import jax.numpy as jnp
from jax import lax
from jax.experimental import pallas as pl
from jax.experimental.pallas import tpu as pltpu
from jax.sharding import PartitionSpec as P

TOK_DEV = 32
LANES = 128
VMEM_ROOM = 48 * 1024 * 1024
MESH = pl.DeviceIdType.MESH


def exchange_body(hidden, down_weight, slot_gate, slot_owner, slot_row, block_count):
    columns = lax.axis_size("ep")
    slot_total = hidden.shape[2]
    send = slot_total // columns
    product = jnp.dot(hidden[0, 0], down_weight[0], preferred_element_type=jnp.float32)
    within = jnp.arange(slot_total) % send
    limits = jnp.repeat(block_count[0, 0], send)
    live = (within < limits).astype(jnp.float32)
    scaled = (product * (slot_gate[0, 0] * live)[:, None]).astype(jnp.bfloat16)
    local_index = slot_owner[0, 0] * TOK_DEV + slot_row[0, 0]
    arrived, arrived_index = (
        lax.all_to_all(scaled, "ep", split_axis=0, concat_axis=0, tiled=True),
        lax.all_to_all(local_index, "ep", split_axis=0, concat_axis=0, tiled=True),
    )
    wanted = jnp.arange(lax.axis_size("grp") * TOK_DEV)
    table = (wanted[:, None] == arrived_index[None, :]).astype(jnp.bfloat16)
    return lax.psum_scatter(
        jnp.dot(table, arrived, preferred_element_type=jnp.float32).astype(jnp.bfloat16),
        "grp",
        scatter_dimension=0,
        tiled=True,
    )


def partner(me, n, k):
    if n & (n - 1):
        return lax.rem(me + n - k, n), lax.rem(me + k, n)
    other, bit = 0, 1
    while bit < n:
        mine = lax.rem(me // bit, 2)
        other = other + bit * (1 - mine if k & bit else mine)
        bit *= 2
    return other, other


def kernel(
    groups, columns, send, piece,
    hidden_ref, weight_ref, gate_ref, owner_ref, row_ref, count_ref, out_ref,
    gate, owner, row, count, sums, result, weight, rows_in, meta, outgoing, arrived, places,
    load_sem, store_sem, weight_sem, hid_send, hid_recv, meta_send, meta_recv,
    row_send, row_recv, place_send, place_recv,
):
    group, column = lax.axis_index("grp"), lax.axis_index("ep")
    slots, width = hidden_ref.shape[2], weight_ref.shape[2]
    pieces = width // piece
    batches = [2 if k == 0 and pieces % 2 == 0 else pieces for k in range(groups)]
    group_steps = list(range(1, groups))
    column_steps = sorted(range(1, columns), key=lambda k: (k % 2, -k)) if columns > 1 else []

    def weight_copy(j):
        cols = pl.ds(j * piece, piece)
        return pltpu.make_async_copy(
            weight_ref.at[0, :, cols], weight.at[:, cols], weight_sem.at[j]
        )

    def result_copy(j):
        cols = pl.ds(j * piece, piece)
        return pltpu.make_async_copy(result.at[:, cols], out_ref.at[:, cols], store_sem.at[j])

    barrier = pltpu.get_barrier_semaphore()
    for k in group_steps:
        pl.semaphore_signal(
            barrier, inc=1, device_id=(partner(group, groups, k)[0], column), device_id_type=MESH
        )
    for k in column_steps:
        pl.semaphore_signal(
            barrier, inc=1, device_id=(group, partner(column, columns, k)[0]), device_id_type=MESH
        )

    loads = [
        pltpu.make_async_copy(gate_ref.at[0], gate, load_sem.at[0]),
        pltpu.make_async_copy(owner_ref.at[0], owner, load_sem.at[1]),
        pltpu.make_async_copy(row_ref.at[0], row, load_sem.at[2]),
        pltpu.make_async_copy(count_ref.at[0], count, load_sem.at[3]),
        pltpu.make_async_copy(hidden_ref.at[0, 0], rows_in.at[0], load_sem.at[4]),
    ]
    for load in loads:
        load.start()
    for j in range(pieces):
        weight_copy(j).start()

    for load in loads:
        load.wait()
    lane = lax.broadcasted_iota(jnp.int32, (1, slots), 1)
    limit = jnp.zeros((1, slots), jnp.int32)
    for q in range(columns):
        limit = jnp.where(lane // send == q, count[:, q:q + 1], limit)
    scale = jnp.where(lane % send < limit, gate[...], 0.0)
    meta[0] = jnp.zeros(meta.shape[1:], jnp.float32)
    meta[0, 0, :, :slots] = scale
    meta[0, 1, :, :slots] = (owner[...] * TOK_DEV + row[...]).astype(jnp.float32)

    pl.semaphore_wait(barrier, groups + columns - 2)

    def hidden_copy(k):
        return pltpu.make_async_remote_copy(
            src_ref=rows_in.at[0], dst_ref=rows_in.at[k],
            send_sem=hid_send.at[k], recv_sem=hid_recv.at[k],
            device_id=(partner(group, groups, k)[0], column), device_id_type=MESH,
        )

    def meta_copy(k):
        return pltpu.make_async_remote_copy(
            src_ref=meta.at[0], dst_ref=meta.at[k],
            send_sem=meta_send.at[k], recv_sem=meta_recv.at[k],
            device_id=(partner(group, groups, k)[0], column), device_id_type=MESH,
        )

    def row_copy(k, m, j):
        to = partner(column, columns, m)[0]
        cols = pl.ds(j * piece, batches[k] * piece)
        return pltpu.make_async_remote_copy(
            src_ref=outgoing.at[k, to, :, cols], dst_ref=arrived.at[k, column, :, cols],
            send_sem=row_send.at[k], recv_sem=row_recv.at[k],
            device_id=(group, to), device_id_type=MESH,
        )

    def place_copy(k, m):
        return pltpu.make_async_remote_copy(
            src_ref=meta.at[k, 1], dst_ref=places.at[k, column],
            send_sem=place_send.at[k], recv_sem=place_recv.at[k],
            device_id=(group, partner(column, columns, m)[0]), device_id_type=MESH,
        )

    def all_rows(k):
        return pltpu.make_async_remote_copy(
            src_ref=outgoing.at[k, pl.ds(0, columns - 1)],
            dst_ref=arrived.at[k, pl.ds(0, columns - 1)],
            send_sem=row_send.at[k], recv_sem=row_recv.at[k],
            device_id=(group, partner(column, columns, 1)[0]), device_id_type=MESH,
        )

    def all_places(k):
        return pltpu.make_async_remote_copy(
            src_ref=places.at[k, pl.ds(0, columns - 1)],
            dst_ref=places.at[k, pl.ds(0, columns - 1)],
            send_sem=place_send.at[k], recv_sem=place_recv.at[k],
            device_id=(group, partner(column, columns, 1)[0]), device_id_type=MESH,
        )

    for k in group_steps:
        meta_copy(k).start()
        hidden_copy(k).start()

    eye = lax.broadcasted_iota(jnp.int32, (slots, slots), 0) == lax.broadcasted_iota(
        jnp.int32, (slots, slots), 1
    )
    for k in range(groups):
        if k:
            meta_copy(k).wait_recv()
            hidden_copy(k).wait_recv()
        for m in column_steps:
            place_copy(k, m).start()
        places[k, column] = meta[k, 1]
        factor = jnp.sum(jnp.where(eye, meta[k, 0, :, :slots], 0.0), axis=1, keepdims=True)
        for j in range(pieces):
            if k == 0:
                weight_copy(j).wait()
            cols = slice(j * piece, (j + 1) * piece)
            product = jnp.dot(rows_in[k], weight[:, cols], preferred_element_type=jnp.float32)
            scaled = product * factor
            for q in range(columns):
                outgoing[k, q, :, cols] = scaled[q * send:(q + 1) * send].astype(jnp.bfloat16)
            if (j + 1) % batches[k] == 0:
                for m in column_steps:
                    row_copy(k, m, j + 1 - batches[k]).start()
        arrived[k, column] = outgoing[k, column]

    total = columns * send
    picked = lax.broadcasted_iota(jnp.int32, (meta.shape[3], total), 0) == (
        column * send + lax.broadcasted_iota(jnp.int32, (meta.shape[3], total), 1) % send
    )
    picked = picked.astype(jnp.float32)
    mine = lax.broadcasted_iota(jnp.int32, (columns, total), 0) == (
        lax.broadcasted_iota(jnp.int32, (columns, total), 1) // send
    )
    wanted = (
        group * TOK_DEV + lax.broadcasted_iota(jnp.int32, (TOK_DEV, total), 0)
    ).astype(jnp.float32)
    tables = []
    for k in range(groups):
        if column_steps:
            all_places(k).wait_recv()
        index = jnp.dot(
            places[k, :, 0], picked,
            precision=lax.Precision.HIGHEST, preferred_element_type=jnp.float32,
        )
        index = jnp.sum(jnp.where(mine, index, 0.0), axis=0, keepdims=True)
        tables.append((wanted == index).astype(jnp.bfloat16))
    for k in range(groups):
        if column_steps:
            all_rows(k).wait_recv()
        for j in range(pieces):
            cols = slice(j * piece, (j + 1) * piece)
            block = jnp.concatenate([arrived[k, e, :, cols] for e in range(columns)], axis=0)
            rows = jnp.dot(tables[k], block, preferred_element_type=jnp.float32)
            if k:
                rows = sums[:, cols] + rows
            if k < groups - 1:
                sums[:, cols] = rows
            else:
                result[:, cols] = rows.astype(out_ref.dtype)
                result_copy(j).start()

    for k in group_steps:
        meta_copy(k).wait_send()
        hidden_copy(k).wait_send()
    for k in range(groups):
        if column_steps:
            all_places(k).wait_send()
            all_rows(k).wait_send()
    for j in range(pieces):
        result_copy(j).wait()


def kernel_body(hidden, down_weight, slot_gate, slot_owner, slot_row, block_count):
    groups, columns = lax.axis_size("grp"), lax.axis_size("ep")
    slots, depth = hidden.shape[2:]
    width = down_weight.shape[2]
    send = slots // columns
    lanes = -(-slots // LANES) * LANES
    piece = 1024 if width % 1024 == 0 else width
    hbm = pl.BlockSpec(memory_space=pltpu.HBM)
    dma = pltpu.SemaphoreType.DMA
    return pl.pallas_call(
        functools.partial(kernel, groups, columns, send, piece),
        out_shape=jax.ShapeDtypeStruct((TOK_DEV, width), jnp.bfloat16),
        in_specs=[hbm] * 6,
        out_specs=hbm,
        scratch_shapes=[
            pltpu.VMEM((1, slots), jnp.float32),
            pltpu.VMEM((1, slots), jnp.int32),
            pltpu.VMEM((1, slots), jnp.int32),
            pltpu.VMEM((1, columns), jnp.int32),
            pltpu.VMEM((TOK_DEV, width), jnp.float32),
            pltpu.VMEM((TOK_DEV, width), jnp.bfloat16),
            pltpu.VMEM((depth, width), jnp.bfloat16),
            pltpu.VMEM((groups, slots, depth), jnp.bfloat16),
            pltpu.VMEM((groups, 2, 1, lanes), jnp.float32),
            pltpu.VMEM((groups, columns, send, width), jnp.bfloat16),
            pltpu.VMEM((groups, columns, send, width), jnp.bfloat16),
            pltpu.VMEM((groups, columns, 1, lanes), jnp.float32),
            dma((5,)), dma((width // piece,)), dma((width // piece,)),
            dma((groups,)), dma((groups,)), dma((groups,)), dma((groups,)),
            dma((groups,)), dma((groups,)), dma((groups,)), dma((groups,)),
        ],
        compiler_params=pltpu.CompilerParams(
            collective_id=0, has_side_effects=True, vmem_limit_bytes=56 * 1024 * 1024
        ),
    )(hidden, down_weight, slot_gate, slot_owner, slot_row, block_count)


def body(hidden, down_weight, *slot_data):
    groups, columns = lax.axis_size("grp"), lax.axis_size("ep")
    slots, depth = hidden.shape[2:]
    width = down_weight.shape[2]
    held = 2 * (depth * width + groups * slots * (depth + 2 * width))
    chosen = kernel_body if held <= VMEM_ROOM else exchange_body
    return chosen(hidden, down_weight, *slot_data)


def solution(mesh):
    in_specs = (
        P("grp", "ep", None, None),
        P("ep", None, None),
        P("grp", "ep", None),
        P("grp", "ep", None),
        P("grp", "ep", None),
        P("grp", "ep", None),
    )
    out_specs = P(("grp", "ep"), None)
    return jax.shard_map(body, mesh=mesh, in_specs=in_specs, out_specs=out_specs, check_vma=False)
```

profile of v0, /device:TPU:0, one launch (start us, length us, event | category | flops | bytes accessed | tf_op | source)
XLA Modules:
  0.0 22.9 jit_solution(5214745632213083028)
XLA Ops:
  0.0 21.3 %shard_map.64 = bf16[32,4096]{1,0:T(8,128)(2,1)} custom-call(bf16[1,1,32,1024]{3,2,1,0:T(8,128)(2,1)} %hidden_ref.1, bf16[1,1024,4096]{2,1,0:T(8,128)(2,1)} %weight_ref.1, f32[1,1,32]{2,1,0:T(1,128)} %gate_ref.1, s32[1,1,32]{2,1,0:T(1,128)} %owner_ref.1, s32[1,1,32]{2,1,0:T(1,128)} %row_ref.1, s32[1,1,8]{2,1,0:T(1,128)} %count_ref.1), custom_call_target="tpu_custom_call" | custom-call | tf_op jit(solution)/shard_map/pallas_call | solution.py:240
  21.3 1.7 %copy.8 = bf16[32,4096]{1,0:T(8,128)(2,1)} copy(bf16[32,4096]{1,0:T(8,128)(2,1)} %shard_map.64) | data formatting | bytes 524288
where the time goes:
time: 23.1 us; the launch traced here: 22.9 us
  Pallas kernels  21.3 us (92%)
  local copies, waits for them, and re-layouts  1.67 us (7%)
    pallas_call x1, Pallas kernels, kernel_body(): pl.pallas_call(functools.partial(kernel, groups, columns, send, piece), o...  21.3 us
    unnamed x1, local copies, waits for them, and re-layouts  1.67 us

commit v1 on v0

v1 whole, which is shorter than its diff:
```python
import functools

import jax
import jax.numpy as jnp
from jax import lax
from jax.experimental import pallas as pl
from jax.experimental.pallas import tpu as pltpu
from jax.sharding import PartitionSpec as P

TOK_DEV = 32
LANES = 128
VMEM_ROOM = 48 * 1024 * 1024
MESH = pl.DeviceIdType.MESH


def exchange_body(hidden, down_weight, slot_gate, slot_owner, slot_row, block_count):
    columns = lax.axis_size("ep")
    slot_total = hidden.shape[2]
    send = slot_total // columns
    product = jnp.dot(hidden[0, 0], down_weight[0], preferred_element_type=jnp.float32)
    within = jnp.arange(slot_total) % send
    limits = jnp.repeat(block_count[0, 0], send)
    live = (within < limits).astype(jnp.float32)
    scaled = (product * (slot_gate[0, 0] * live)[:, None]).astype(jnp.bfloat16)
    local_index = slot_owner[0, 0] * TOK_DEV + slot_row[0, 0]
    arrived, arrived_index = (
        lax.all_to_all(scaled, "ep", split_axis=0, concat_axis=0, tiled=True),
        lax.all_to_all(local_index, "ep", split_axis=0, concat_axis=0, tiled=True),
    )
    wanted = jnp.arange(lax.axis_size("grp") * TOK_DEV)
    table = (wanted[:, None] == arrived_index[None, :]).astype(jnp.bfloat16)
    return lax.psum_scatter(
        jnp.dot(table, arrived, preferred_element_type=jnp.float32).astype(jnp.bfloat16),
        "grp",
        scatter_dimension=0,
        tiled=True,
    )


def partner(me, n, k):
    if n & (n - 1):
        return lax.rem(me + n - k, n), lax.rem(me + k, n)
    other, bit = 0, 1
    while bit < n:
        mine = lax.rem(me // bit, 2)
        other = other + bit * (1 - mine if k & bit else mine)
        bit *= 2
    return other, other


def source_at(group, groups, step):
    if step == 0:
        return group
    if step == 1:
        return group + 1 - 2 * lax.rem(group, 2)
    lower = group < groups // 2
    place = jnp.where(lower, group, groups - 1 - group)
    base = place - lax.rem(place, 2)
    at = jnp.where(base > step - 2, step - 2, step)
    return jnp.where(lower, at, groups - 1 - at)


def kernel(
    groups, columns, send, piece,
    hidden_ref, weight_ref, gate_ref, owner_ref, row_ref, count_ref,
    sums, last_rows, last_table,
    gate, owner, row, count, weight, rows_in, meta, outgoing, arrived, places,
    load_sem, weight_sem, ready, hid_send, hid_recv, meta_send, meta_recv,
    row_send, row_recv, place_send, place_recv,
):
    group, column = lax.axis_index("grp"), lax.axis_index("ep")
    slots, width = hidden_ref.shape[2], weight_ref.shape[2]
    pieces = width // piece
    last = groups - 1
    batches = [2 if k == 0 and pieces % 2 == 0 else pieces for k in range(groups)]
    sources = [source_at(group, groups, k) for k in range(groups)]
    column_steps = sorted(range(1, columns), key=lambda k: (k % 2, -k)) if columns > 1 else []

    def weight_copy(j):
        cols = pl.ds(j * piece, piece)
        return pltpu.make_async_copy(
            weight_ref.at[0, :, cols], weight.at[:, cols], weight_sem.at[j]
        )

    barrier = pltpu.get_barrier_semaphore()
    for k in column_steps:
        pl.semaphore_signal(
            barrier, inc=1, device_id=(group, partner(column, columns, k)[0]), device_id_type=MESH
        )
    for t in range(groups):

        @pl.when((t > group) | (t == group - 1))
        def greet():
            pl.semaphore_signal(barrier, inc=1, device_id=(t, column), device_id_type=MESH)

    loads = [
        pltpu.make_async_copy(hidden_ref.at[0, 0], rows_in.at[group], load_sem.at[4]),
        pltpu.make_async_copy(gate_ref.at[0], gate, load_sem.at[0]),
        pltpu.make_async_copy(owner_ref.at[0], owner, load_sem.at[1]),
        pltpu.make_async_copy(row_ref.at[0], row, load_sem.at[2]),
        pltpu.make_async_copy(count_ref.at[0], count, load_sem.at[3]),
    ]
    for load in loads:
        load.start()
    for j in range(pieces):
        weight_copy(j).start()

    for load in loads:
        load.wait()
    lane = lax.broadcasted_iota(jnp.int32, (1, slots), 1)
    limit = jnp.zeros((1, slots), jnp.int32)
    for q in range(columns):
        limit = jnp.where(lane // send == q, count[:, q:q + 1], limit)
    scale = jnp.where(lane % send < limit, gate[...], 0.0)
    meta[group] = jnp.zeros(meta.shape[1:], jnp.float32)
    meta[group, 0, :, :slots] = scale
    meta[group, 1, :, :slots] = (owner[...] * TOK_DEV + row[...]).astype(jnp.float32)

    pl.semaphore_wait(barrier, columns - 1 + group + jnp.where(group < last, 1, 0))

    def hidden_copy(at, to):
        return pltpu.make_async_remote_copy(
            src_ref=rows_in.at[at], dst_ref=rows_in.at[at],
            send_sem=hid_send.at[to], recv_sem=hid_recv.at[at],
            device_id=(to, column), device_id_type=MESH,
        )

    def meta_copy(at, to):
        return pltpu.make_async_remote_copy(
            src_ref=meta.at[at], dst_ref=meta.at[at],
            send_sem=meta_send.at[to], recv_sem=meta_recv.at[at],
            device_id=(to, column), device_id_type=MESH,
        )

    def rows_at(k):
        return last_rows if k == last else arrived.at[k]

    def row_copy(k, m, j):
        to = partner(column, columns, m)[0]
        cols = pl.ds(j * piece, batches[k] * piece)
        return pltpu.make_async_remote_copy(
            src_ref=outgoing.at[k, to, :, cols], dst_ref=rows_at(k).at[column, :, cols],
            send_sem=row_send.at[k], recv_sem=row_recv.at[k],
            device_id=(group, to), device_id_type=MESH,
        )

    def place_copy(m):
        return pltpu.make_async_remote_copy(
            src_ref=meta.at[:, 1], dst_ref=places.at[column],
            send_sem=place_send, recv_sem=place_recv,
            device_id=(group, partner(column, columns, m)[0]), device_id_type=MESH,
        )

    def all_rows(k):
        return pltpu.make_async_remote_copy(
            src_ref=outgoing.at[k, pl.ds(0, columns - 1)],
            dst_ref=rows_at(k).at[pl.ds(0, columns - 1)],
            send_sem=row_send.at[k], recv_sem=row_recv.at[k],
            device_id=(group, partner(column, columns, 1)[0]), device_id_type=MESH,
        )

    def all_places():
        return pltpu.make_async_remote_copy(
            src_ref=places.at[pl.ds(0, columns - 1)],
            dst_ref=places.at[pl.ds(0, columns - 1)],
            send_sem=place_send, recv_sem=place_recv,
            device_id=(group, partner(column, columns, 1)[0]), device_id_type=MESH,
        )

    def share(to):
        meta_copy(group, to).start()
        hidden_copy(group, to).start()

    if groups > 1:
        share(sources[1])
    for t in range(groups):

        @pl.when((t < group) & (t != sources[min(1, groups - 1)]) | (t == group + 1) & (lax.rem(group, 2) == 1))
        def share_near():
            share(t)

        @pl.when(t < group - 1)
        def say_ready():
            pl.semaphore_signal(
                ready.at[group], inc=1, device_id=(t, column), device_id_type=MESH
            )

    def share_far(to):
        @pl.when(to < groups)
        def wait_and_share():
            pl.semaphore_wait(ready.at[to], 1)
            share(to)

    eye = lax.broadcasted_iota(jnp.int32, (slots, slots), 0) == lax.broadcasted_iota(
        jnp.int32, (slots, slots), 1
    )
    for k in range(groups):
        if k:
            meta_copy(sources[k], sources[k]).wait_recv()
            hidden_copy(sources[k], sources[k]).wait_recv()
        if k == last:
            for m in column_steps:
                place_copy(m).start()
            places[column] = meta[:, 1]
        factor = jnp.sum(jnp.where(eye, meta[sources[k], 0, :, :slots], 0.0), axis=1, keepdims=True)
        for j in range(pieces):
            if k == 0:
                weight_copy(j).wait()
            cols = slice(j * piece, (j + 1) * piece)
            product = jnp.dot(rows_in[sources[k]], weight[:, cols], preferred_element_type=jnp.float32)
            scaled = product * factor
            for q in range(columns):
                outgoing[k, q, :, cols] = scaled[q * send:(q + 1) * send].astype(jnp.bfloat16)
            if (j + 1) % batches[k] == 0:
                for m in column_steps:
                    row_copy(k, m, j + 1 - batches[k]).start()
        rows_at(k)[column] = outgoing[k, column]
        share_far(group + 2 + k)

    total = columns * send
    lanes = meta.shape[3]
    picked = lax.broadcasted_iota(jnp.int32, (lanes, total), 0) == (
        column * send + lax.broadcasted_iota(jnp.int32, (lanes, total), 1) % send
    )
    picked = picked.astype(jnp.float32)
    mine = lax.broadcasted_iota(jnp.int32, (columns, total), 0) == (
        lax.broadcasted_iota(jnp.int32, (columns, total), 1) // send
    )
    wanted = (
        group * TOK_DEV + lax.broadcasted_iota(jnp.int32, (TOK_DEV, total), 0)
    ).astype(jnp.float32)
    if column_steps:
        all_places().wait_recv()
    tables = []
    for k in range(groups):
        index = jnp.dot(
            places[:, sources[k], 0], picked,
            precision=lax.Precision.HIGHEST, preferred_element_type=jnp.float32,
        )
        index = jnp.sum(jnp.where(mine, index, 0.0), axis=0, keepdims=True)
        tables.append((wanted == index).astype(jnp.bfloat16))
    last_table[...] = tables[last]
    for k in range(last):
        if column_steps:
            all_rows(k).wait_recv()
        for j in range(pieces):
            cols = slice(j * piece, (j + 1) * piece)
            block = jnp.concatenate([arrived[k, e, :, cols] for e in range(columns)], axis=0)
            rows = jnp.dot(tables[k], block, preferred_element_type=jnp.float32)
            sums[:, cols] = sums[:, cols] + rows if k else rows
    if not last:
        sums[...] = jnp.zeros(sums.shape, jnp.float32)

    for k in range(1, groups):
        meta_copy(group, sources[k]).wait_send()
        hidden_copy(group, sources[k]).wait_send()
    if column_steps:
        all_places().wait_send()
        for k in range(groups):
            all_rows(k).wait_send()
        all_rows(last).wait_recv()


def finish(piece, sums, last_rows, last_table, out_ref, result, store_sem):
    columns, width = last_rows.shape[0], last_rows.shape[2]
    copies = []
    for j in range(width // piece):
        cols = slice(j * piece, (j + 1) * piece)
        block = jnp.concatenate([last_rows[e, :, cols] for e in range(columns)], axis=0)
        rows = jnp.dot(last_table[...], block, preferred_element_type=jnp.float32)
        result[:, cols] = (sums[:, cols] + rows).astype(out_ref.dtype)
        copy = pltpu.make_async_copy(
            result.at[:, cols], out_ref.at[:, cols], store_sem.at[j]
        )
        copy.start()
        copies.append(copy)
    for copy in copies:
        copy.wait()


def kernel_body(hidden, down_weight, slot_gate, slot_owner, slot_row, block_count):
    groups, columns = lax.axis_size("grp"), lax.axis_size("ep")
    slots, depth = hidden.shape[2:]
    width = down_weight.shape[2]
    send = slots // columns
    lanes = -(-slots // LANES) * LANES
    piece = 1024 if width % 1024 == 0 else width
    pieces = width // piece
    hbm = pl.BlockSpec(memory_space=pltpu.HBM)
    vmem = pl.BlockSpec(memory_space=pltpu.VMEM)
    dma = pltpu.SemaphoreType.DMA
    held = pl.pallas_call(
        functools.partial(kernel, groups, columns, send, piece),
        out_shape=(
            pltpu.VMEM((TOK_DEV, width), jnp.float32),
            pltpu.VMEM((columns, send, width), jnp.bfloat16),
            pltpu.VMEM((TOK_DEV, columns * send), jnp.bfloat16),
        ),
        in_specs=[hbm] * 6,
        out_specs=(vmem,) * 3,
        scratch_shapes=[
            pltpu.VMEM((1, slots), jnp.float32),
            pltpu.VMEM((1, slots), jnp.int32),
            pltpu.VMEM((1, slots), jnp.int32),
            pltpu.VMEM((1, columns), jnp.int32),
            pltpu.VMEM((depth, width), jnp.bfloat16),
            pltpu.VMEM((groups, slots, depth), jnp.bfloat16),
            pltpu.VMEM((groups, 2, 1, lanes), jnp.float32),
            pltpu.VMEM((groups, columns, send, width), jnp.bfloat16),
            pltpu.VMEM((max(groups - 1, 1), columns, send, width), jnp.bfloat16),
            pltpu.VMEM((columns, groups, 1, lanes), jnp.float32),
            dma((5,)), dma((pieces,)), pltpu.SemaphoreType.REGULAR((groups,)),
            dma((groups,)), dma((groups,)), dma((groups,)), dma((groups,)),
            dma((groups,)), dma((groups,)), dma, dma,
        ],
        compiler_params=pltpu.CompilerParams(
            collective_id=0, has_side_effects=True, vmem_limit_bytes=60 * 1024 * 1024
        ),
    )(hidden, down_weight, slot_gate, slot_owner, slot_row, block_count)
    return pl.pallas_call(
        functools.partial(finish, piece),
        out_shape=jax.ShapeDtypeStruct((TOK_DEV, width), jnp.bfloat16),
        in_specs=[vmem] * 3,
        out_specs=hbm,
        scratch_shapes=[pltpu.VMEM((TOK_DEV, width), jnp.bfloat16), dma((pieces,))],
        compiler_params=pltpu.CompilerParams(vmem_limit_bytes=8 * 1024 * 1024),
    )(*held)


def body(hidden, down_weight, *slot_data):
    groups, columns = lax.axis_size("grp"), lax.axis_size("ep")
    slots, depth = hidden.shape[2:]
    width = down_weight.shape[2]
    held = 2 * (depth * width + groups * slots * (depth + 2 * width))
    fits = held <= VMEM_ROOM and groups % 2 == 0
    chosen = kernel_body if fits else exchange_body
    return chosen(hidden, down_weight, *slot_data)


def solution(mesh):
    in_specs = (
        P("grp", "ep", None, None),
        P("ep", None, None),
        P("grp", "ep", None),
        P("grp", "ep", None),
        P("grp", "ep", None),
        P("grp", "ep", None),
    )
    out_specs = P(("grp", "ep"), None)
    return jax.shard_map(body, mesh=mesh, in_specs=in_specs, out_specs=out_specs, check_vma=False)
```

time: 23.1 us -> 21.6 us (0.935)
  local copies, waits for them, and re-layouts: 1.67 us -> 0 us
    unnamed x1 -> x0, local copies, waits for them, and re-layouts: 1.67 us -> none
    pallas_call x0 -> x1, Pallas kernels: none -> 0.89 us  [kernel_body(): pl.pallas_call(functools.partial(finish, piece), out_shape=jax.ShapeDtype...]
    pallas_call x1, Pallas kernels: 21.3 us -> 20.5 us  [kernel_body(): pl.pallas_call(functools.partial(kernel, groups, columns, send, piece), o...]
where the time goes in v1:
time: 21.6 us; the launch traced here: 21.4 us
  Pallas kernels  21.4 us (99%)
    pallas_call x1, Pallas kernels, kernel_body(): pl.pallas_call(functools.partial(kernel, groups, columns, send, piece), o...  20.5 us
    pallas_call x1, Pallas kernels, kernel_body(): pl.pallas_call(functools.partial(finish, piece), out_shape=jax.ShapeDtype...  0.89 us

profile of v1, /device:TPU:0, one launch (start us, length us, event | category | flops | bytes accessed | tf_op | source)
XLA Modules:
  0.0 21.4 jit_solution(8061943752814268079)
XLA Ops:
  0.0 20.5 %shard_map.64 = (f32[32,4096]{1,0:T(8,128)S(1)}, bf16[8,4,4096]{2,1,0:T(4,128)(2,1)S(1)}, bf16[32,32]{1,0:T(8,128)(2,1)S(1)}) custom-call(bf16[1,1,32,1024]{3,2,1,0:T(8,128)(2,1)} %hidden_ref.1, bf16[1,1024,4096]{2,1,0:T(8,128)(2,1)} %weight_ref.1, f32[1,1,32]{2,1,0:T(1,128)} %gate_ref.1, s32[1,1,32]{2,1,0:T(1,128)} %owner_ref.1, s32[1,1,32]{2,1,0:T(1,128)} %row_ref.1, ...), custom_call_target="tpu_custom_call" | custom-call | tf_op jit(solution)/shard_map/pallas_call | solution.py:292
  20.5 0.9 %shard_map.65 = bf16[32,4096]{1,0:T(8,128)(2,1)} custom-call(f32[32,4096]{1,0:T(8,128)S(1)} %get-tuple-element.8.sums, bf16[8,4,4096]{2,1,0:T(4,128)(2,1)S(1)} %get-tuple-element.9.last_rows, bf16[32,32]{1,0:T(8,128)(2,1)S(1)} %get-tuple-element.10.last_table), custom_call_target="tpu_custom_call" | custom-call | tf_op jit(solution)/shard_map/pallas_call | solution.py:320

commit v2 on v1

v2 whole, which is shorter than its diff:
```python
import functools

import jax
import jax.numpy as jnp
from jax import lax
from jax.experimental import pallas as pl
from jax.experimental.pallas import tpu as pltpu
from jax.sharding import PartitionSpec as P

TOK_DEV = 32
LANES = 128
PIECE = 1024
PLANES = 4
VMEM_ROOM = 48 * 1024 * 1024
MESH = pl.DeviceIdType.MESH


def exchange_body(hidden, down_weight, slot_gate, slot_owner, slot_row, block_count):
    columns = lax.axis_size("ep")
    slot_total = hidden.shape[2]
    send = slot_total // columns
    product = jnp.dot(hidden[0, 0], down_weight[0], preferred_element_type=jnp.float32)
    within = jnp.arange(slot_total) % send
    limits = jnp.repeat(block_count[0, 0], send)
    live = (within < limits).astype(jnp.float32)
    scaled = (product * (slot_gate[0, 0] * live)[:, None]).astype(jnp.bfloat16)
    local_index = slot_owner[0, 0] * TOK_DEV + slot_row[0, 0]
    arrived, arrived_index = (
        lax.all_to_all(scaled, "ep", split_axis=0, concat_axis=0, tiled=True),
        lax.all_to_all(local_index, "ep", split_axis=0, concat_axis=0, tiled=True),
    )
    wanted = jnp.arange(lax.axis_size("grp") * TOK_DEV)
    table = (wanted[:, None] == arrived_index[None, :]).astype(jnp.bfloat16)
    return lax.psum_scatter(
        jnp.dot(table, arrived, preferred_element_type=jnp.float32).astype(jnp.bfloat16),
        "grp",
        scatter_dimension=0,
        tiled=True,
    )


def partner(me, n, k):
    if n & (n - 1):
        return lax.rem(me + n - k, n), lax.rem(me + k, n)
    other, bit = 0, 1
    while bit < n:
        mine = lax.rem(me // bit, 2)
        other = other + bit * (1 - mine if k & bit else mine)
        bit *= 2
    return other, other


def local_cols(group, width, start, size):
    at = lax.rem(start + lax.rem(group, 2) * (width // 2), width)
    return pl.ds(pl.multiple_of(at, size), size)


def kernel(
    groups, columns, send, piece,
    hidden_ref, weight_ref, gate_ref, owner_ref, row_ref, count_ref,
    sums, last_rows, last_table,
    gate, owner, row, count, weight, rows_in, meta,
    out_early, out_late, in_early, in_late, pair_places, places, swap_out, swap_in,
    load_sem, weight_sem, hid_send, hid_recv, meta_send, meta_recv,
    row_send, row_recv, place_send, place_recv, swap_send, swap_recv,
):
    group, column = lax.axis_index("grp"), lax.axis_index("ep")
    slots, width = hidden_ref.shape[2], weight_ref.shape[2]
    half = width // 2
    last = groups - 1
    total = columns * send
    pair = group + 1 - 2 * lax.rem(group, 2)
    pair_base = group - lax.rem(group, 2)
    far, far_pair = last - group, last - pair
    end = group == last
    sources = [group, pair, jnp.where(end, far_pair, far), jnp.where(end, far, far_pair)]
    column_steps = sorted(range(1, columns), key=lambda k: (k % 2, -k))

    def weight_copy(j):
        return pltpu.make_async_copy(
            weight_ref.at[0, :, local_cols(group, width, j * piece, piece)],
            weight.at[:, pl.ds(j * piece, piece)],
            weight_sem.at[j],
        )

    loads = [
        pltpu.make_async_copy(hidden_ref.at[0, 0], rows_in.at[group], load_sem.at[4]),
        pltpu.make_async_copy(gate_ref.at[0], gate, load_sem.at[0]),
        pltpu.make_async_copy(owner_ref.at[0], owner, load_sem.at[1]),
        pltpu.make_async_copy(row_ref.at[0], row, load_sem.at[2]),
        pltpu.make_async_copy(count_ref.at[0], count, load_sem.at[3]),
    ]
    for load in loads:
        load.start()

    barrier = pltpu.get_barrier_semaphore()
    for k in column_steps:
        pl.semaphore_signal(
            barrier, inc=1, device_id=(group, partner(column, columns, k)[0]), device_id_type=MESH
        )
    pl.semaphore_signal(barrier, inc=1, device_id=(pair, column), device_id_type=MESH)

    @pl.when(group < last)
    def greet_far():
        pl.semaphore_signal(barrier, inc=1, device_id=(far, column), device_id_type=MESH)

    for load in loads:
        load.wait()
    for j in range(width // piece):
        weight_copy(j).start()
    lane = lax.broadcasted_iota(jnp.int32, (1, slots), 1)
    limit = jnp.zeros((1, slots), jnp.int32)
    for q in range(columns):
        limit = jnp.where(lane // send == q, count[:, q:q + 1], limit)
    scale = jnp.where(lane % send < limit, gate[...], 0.0)
    meta[group] = jnp.zeros(meta.shape[1:], jnp.float32)
    meta[group, 0, :, :slots] = scale
    meta[group, 1, :, :slots] = (owner[...] * TOK_DEV + row[...]).astype(jnp.float32)

    pl.semaphore_wait(barrier, columns + jnp.where(group > 0, 1, 0))

    def share_copies(at, to, slot=None):
        slot = at if slot is None else slot
        return [
            pltpu.make_async_remote_copy(
                src_ref=held.at[at], dst_ref=held.at[at],
                send_sem=sent.at[slot], recv_sem=landed.at[at],
                device_id=(to, column), device_id_type=MESH,
            )
            for held, sent, landed in ((meta, meta_send, meta_recv), (rows_in, hid_send, hid_recv))
        ]

    def share(at, to, slot=None):
        for copy in share_copies(at, to, slot):
            copy.start()

    def wait_shared(at):
        for copy in share_copies(at, at):
            copy.wait_recv()

    def wait_sent(slot):
        for copy in share_copies(group, pair, slot):
            copy.wait_send()

    def rows_out(k):
        return out_early.at[k] if k < 2 else out_late.at[k - 2]

    def rows_at(k):
        return in_early.at[k] if k < 2 else last_rows if k == last else in_late.at[k - 2]

    def row_copy(k, m, j, batch):
        to = partner(column, columns, m)[0]
        cols = pl.ds(j * piece, batch * piece)
        return pltpu.make_async_remote_copy(
            src_ref=rows_out(k).at[to, :, cols], dst_ref=rows_at(k).at[column, :, cols],
            send_sem=row_send.at[k], recv_sem=row_recv.at[k],
            device_id=(group, to), device_id_type=MESH,
        )

    def all_rows(k):
        return pltpu.make_async_remote_copy(
            src_ref=rows_out(k).at[pl.ds(0, columns - 1)],
            dst_ref=rows_at(k).at[pl.ds(0, columns - 1)],
            send_sem=row_send.at[k], recv_sem=row_recv.at[k],
            device_id=(group, partner(column, columns, 1)[0]), device_id_type=MESH,
        )

    def place_copy(k, m):
        src = meta.at[sources[k], 1] if k > 1 else meta.at[pl.ds(pair_base, 2), 1]
        dst = places.at[k - 2, column] if k > 1 else pair_places.at[column]
        return pltpu.make_async_remote_copy(
            src_ref=src, dst_ref=dst,
            send_sem=place_send.at[k - 1], recv_sem=place_recv.at[k - 1],
            device_id=(group, partner(column, columns, m)[0]), device_id_type=MESH,
        )

    def all_places(k):
        some = (places.at[k - 2] if k > 1 else pair_places).at[pl.ds(0, columns - 1)]
        return pltpu.make_async_remote_copy(
            src_ref=some, dst_ref=some,
            send_sem=place_send.at[k - 1], recv_sem=place_recv.at[k - 1],
            device_id=(group, partner(column, columns, 1)[0]), device_id_type=MESH,
        )

    def swap_copy(j):
        cols = pl.ds(j * piece, piece)
        return pltpu.make_async_remote_copy(
            src_ref=swap_out.at[:, cols], dst_ref=swap_in.at[:, cols],
            send_sem=swap_send.at[j], recv_sem=swap_recv.at[j],
            device_id=(pair, column), device_id_type=MESH,
        )

    share(group, pair)

    @pl.when(group > 0)
    def share_far():
        share(group, far, groups)

    eye = lax.broadcasted_iota(jnp.int32, (slots, slots), 0) == lax.broadcasted_iota(
        jnp.int32, (slots, slots), 1
    )
    lanes = meta.shape[3]
    picked = lax.broadcasted_iota(jnp.int32, (lanes, total), 0) == (
        column * send + lax.broadcasted_iota(jnp.int32, (lanes, total), 1) % send
    )
    picked = picked.astype(jnp.float32)
    mine = lax.broadcasted_iota(jnp.int32, (columns, total), 0) == (
        lax.broadcasted_iota(jnp.int32, (columns, total), 1) // send
    )
    token = lax.broadcasted_iota(jnp.int32, (TOK_DEV, total), 0)

    def table_of(found, owners):
        index = jnp.dot(
            found, picked, precision=lax.Precision.HIGHEST, preferred_element_type=jnp.float32
        )
        index = jnp.sum(jnp.where(mine, index, 0.0), axis=0, keepdims=True)
        return [
            ((owner_group * TOK_DEV + token).astype(jnp.float32) == index).astype(jnp.bfloat16)
            for owner_group in owners
        ]

    def block(k, cols):
        return jnp.concatenate([rows_at(k)[e, :, cols] for e in range(columns)], axis=0)

    def early_sums():
        all_places(1).wait_recv()
        both = []
        for k in range(2):
            found = pair_places[:, sources[k] - pair_base, 0]
            both.append(jnp.concatenate(table_of(found, (group, pair)), axis=0))
        table = jnp.concatenate(both, axis=1)
        for k in range(2):
            all_rows(k).wait_recv()
        for j in range(half // piece):
            cols = slice(j * piece, (j + 1) * piece)
            rows = jnp.concatenate([block(0, cols), block(1, cols)], axis=0)
            rows = jnp.dot(table, rows, preferred_element_type=jnp.float32)
            swap_out[:, cols] = rows[TOK_DEV:].astype(jnp.bfloat16)
            swap_copy(j).start()
            sums[:, cols] = rows[:TOK_DEV]

    for k in range(groups):
        if k in (1, 2):
            wait_shared(sources[k])

            @pl.when(group == 1 if k == 1 else group < last)
            def forward():
                share(sources[k], far if k == 1 else pair)

        if k == last:

            @pl.when(group != last - 1)
            def wait_last():
                wait_shared(sources[k])

        if k:
            for m in column_steps:
                place_copy(k, m).start()
        if k == 1:
            pair_places[column] = meta[pl.ds(pair_base, 2), 1]
        elif k > 1:
            places[k - 2, column] = meta[sources[k], 1]
        factor = jnp.sum(jnp.where(eye, meta[sources[k], 0, :, :slots], 0.0), axis=1, keepdims=True)
        batch = 1
        for j in range((half if k < 2 else width) // piece):
            if k == 0 or k == 2 and j >= half // piece:
                weight_copy(j).wait()
            cols = slice(j * piece, (j + 1) * piece)
            product = jnp.dot(rows_in[sources[k]], weight[:, cols], preferred_element_type=jnp.float32)
            scaled = product * factor
            for q in range(columns):
                rows_out(k)[q, :, cols] = scaled[q * send:(q + 1) * send].astype(jnp.bfloat16)
            if (j + 1) % batch == 0:
                for m in column_steps:
                    row_copy(k, m, j + 1 - batch, batch).start()
        rows_at(k)[column] = rows_out(k)[column]
        if k == 2:

            @pl.when(group == last - 1)
            def forward_last():
                wait_shared(sources[last])
                share(sources[last], pair)

            early_sums()

    tables = []
    for k in range(2, groups):
        all_places(k).wait_recv()
        tables.append(table_of(places[k - 2, :, 0], (group,))[0])
    last_table[...] = tables[-1]
    for k in range(2, last):
        all_rows(k).wait_recv()
        if k == 2:
            for j in range(half // piece):
                swap_copy(j).wait_recv()
        for j in range(width // piece):
            cols = slice(j * piece, (j + 1) * piece)
            rows = jnp.dot(tables[k - 2], block(k, cols), preferred_element_type=jnp.float32)
            if k > 2 or j < half // piece:
                sums[:, cols] = sums[:, cols] + rows
            else:
                swapped = swap_in[:, j * piece - half:(j + 1) * piece - half]
                sums[:, cols] = swapped.astype(jnp.float32) + rows

    wait_sent(group)

    @pl.when(group > 0)
    def sent_far():
        wait_sent(groups)

    @pl.when(group == 1)
    def sent_first():
        wait_sent(sources[1])

    @pl.when(group < last)
    def sent_second():
        wait_sent(sources[2])

    @pl.when(group == last - 1)
    def sent_last():
        wait_sent(sources[last])

    for k in range(1, groups):
        all_places(k).wait_send()
    for j in range(half // piece):
        swap_copy(j).wait_send()
    all_rows(last).wait_recv()
    for k in range(groups):
        all_rows(k).wait_send()


def finish(piece, sums, last_rows, last_table, out_ref, result, store_sem):
    group = lax.axis_index("grp")
    columns, width = last_rows.shape[0], last_rows.shape[2]
    copies = []
    for j in range(width // piece):
        cols = slice(j * piece, (j + 1) * piece)
        block = jnp.concatenate([last_rows[e, :, cols] for e in range(columns)], axis=0)
        rows = jnp.dot(last_table[...], block, preferred_element_type=jnp.float32)
        result[:, cols] = (sums[:, cols] + rows).astype(out_ref.dtype)
        copy = pltpu.make_async_copy(
            result.at[:, cols],
            out_ref.at[:, local_cols(group, width, j * piece, piece)],
            store_sem.at[j],
        )
        copy.start()
        copies.append(copy)
    for copy in copies:
        copy.wait()


def kernel_body(hidden, down_weight, slot_gate, slot_owner, slot_row, block_count):
    groups, columns = lax.axis_size("grp"), lax.axis_size("ep")
    slots, depth = hidden.shape[2:]
    width = down_weight.shape[2]
    send = slots // columns
    lanes = -(-slots // LANES) * LANES
    pieces, halves = width // PIECE, width // 2 // PIECE
    hbm = pl.BlockSpec(memory_space=pltpu.HBM)
    vmem = pl.BlockSpec(memory_space=pltpu.VMEM)
    dma = pltpu.SemaphoreType.DMA
    held = pl.pallas_call(
        functools.partial(kernel, groups, columns, send, PIECE),
        out_shape=(
            pltpu.VMEM((TOK_DEV, width), jnp.float32),
            pltpu.VMEM((columns, send, width), jnp.bfloat16),
            pltpu.VMEM((TOK_DEV, columns * send), jnp.bfloat16),
        ),
        in_specs=[hbm] * 6,
        out_specs=(vmem,) * 3,
        scratch_shapes=[
            pltpu.VMEM((1, slots), jnp.float32),
            pltpu.VMEM((1, slots), jnp.int32),
            pltpu.VMEM((1, slots), jnp.int32),
            pltpu.VMEM((1, columns), jnp.int32),
            pltpu.VMEM((depth, width), jnp.bfloat16),
            pltpu.VMEM((groups, slots, depth), jnp.bfloat16),
            pltpu.VMEM((groups, 2, 1, lanes), jnp.float32),
            pltpu.VMEM((2, columns, send, width // 2), jnp.bfloat16),
            pltpu.VMEM((groups - 2, columns, send, width), jnp.bfloat16),
            pltpu.VMEM((2, columns, send, width // 2), jnp.bfloat16),
            pltpu.VMEM((groups - 3, columns, send, width), jnp.bfloat16),
            pltpu.VMEM((columns, 2, 1, lanes), jnp.float32),
            pltpu.VMEM((groups - 2, columns, 1, lanes), jnp.float32),
            pltpu.VMEM((TOK_DEV, width // 2), jnp.bfloat16),
            pltpu.VMEM((TOK_DEV, width // 2), jnp.bfloat16),
            dma((5,)), dma((pieces,)),
            dma((groups + 1,)), dma((groups,)), dma((groups + 1,)), dma((groups,)),
            dma((groups,)), dma((groups,)), dma((groups - 1,)), dma((groups - 1,)),
            dma((halves,)), dma((halves,)),
        ],
        compiler_params=pltpu.CompilerParams(
            collective_id=0, has_side_effects=True, vmem_limit_bytes=60 * 1024 * 1024
        ),
    )(hidden, down_weight, slot_gate, slot_owner, slot_row, block_count)
    return pl.pallas_call(
        functools.partial(finish, PIECE),
        out_shape=jax.ShapeDtypeStruct((TOK_DEV, width), jnp.bfloat16),
        in_specs=[vmem] * 3,
        out_specs=hbm,
        scratch_shapes=[pltpu.VMEM((TOK_DEV, width), jnp.bfloat16), dma((pieces,))],
        compiler_params=pltpu.CompilerParams(vmem_limit_bytes=8 * 1024 * 1024),
    )(*held)


def body(hidden, down_weight, *slot_data):
    groups, columns = lax.axis_size("grp"), lax.axis_size("ep")
    slots, depth = hidden.shape[2:]
    width = down_weight.shape[2]
    held = 2 * (depth * width + groups * slots * (depth + 2 * width))
    even = groups == PLANES and columns > 1 and width % (2 * PIECE) == 0
    fits = held <= VMEM_ROOM and even
    chosen = kernel_body if fits else exchange_body
    return chosen(hidden, down_weight, *slot_data)


def solution(mesh):
    in_specs = (
        P("grp", "ep", None, None),
        P("ep", None, None),
        P("grp", "ep", None),
        P("grp", "ep", None),
        P("grp", "ep", None),
        P("grp", "ep", None),
    )
    out_specs = P(("grp", "ep"), None)
    return jax.shard_map(body, mesh=mesh, in_specs=in_specs, out_specs=out_specs, check_vma=False)
```

time: 21.6 us -> 20 us (0.926)
  Pallas kernels: 21.4 us -> 19.8 us
    pallas_call x2, Pallas kernels: 21.4 us -> 19.8 us  [the longest x1 18.9 us: kernel_body(): pl.pallas_call(functools.partial(kernel, groups, columns, send, PIECE), o...]
where the time goes in v2:
time: 20 us; the launch traced here: 19.8 us
  Pallas kernels  19.8 us (99%)
    pallas_call x1, Pallas kernels, kernel_body(): pl.pallas_call(functools.partial(kernel, groups, columns, send, PIECE), o...  18.9 us
    pallas_call x1, Pallas kernels, kernel_body(): pl.pallas_call(functools.partial(finish, PIECE), out_shape=jax.ShapeDtype...  0.89 us

profile of v2, /device:TPU:0, one launch (start us, length us, event | category | flops | bytes accessed | tf_op | source)
XLA Modules:
  0.0 19.8 jit_solution(6290906099742007441)
XLA Ops:
  0.0 18.9 %shard_map.64 = (f32[32,4096]{1,0:T(8,128)S(1)}, bf16[8,4,4096]{2,1,0:T(4,128)(2,1)S(1)}, bf16[32,32]{1,0:T(8,128)(2,1)S(1)}) custom-call(bf16[1,1,32,1024]{3,2,1,0:T(8,128)(2,1)} %hidden_ref.1, bf16[1,1024,4096]{2,1,0:T(8,128)(2,1)} %weight_ref.1, f32[1,1,32]{2,1,0:T(1,128)} %gate_ref.1, s32[1,1,32]{2,1,0:T(1,128)} %owner_ref.1, s32[1,1,32]{2,1,0:T(1,128)} %row_ref.1, ...), custom_call_target="tpu_custom_call" | custom-call | tf_op jit(solution)/shard_map/pallas_call | solution.py:362
  18.9 0.9 %shard_map.65 = bf16[32,4096]{1,0:T(8,128)(2,1)} custom-call(f32[32,4096]{1,0:T(8,128)S(1)} %get-tuple-element.8.sums, bf16[8,4,4096]{2,1,0:T(4,128)(2,1)S(1)} %get-tuple-element.9.last_rows, bf16[32,32]{1,0:T(8,128)(2,1)S(1)} %get-tuple-element.10.last_table), custom_call_target="tpu_custom_call" | custom-call | tf_op jit(solution)/shard_map/pallas_call | solution.py:396

commit v3 on v2

--- a/solution.py
+++ b/solution.py
@@ -190,12 +190,11 @@
             device_id=(pair, column), device_id_type=MESH,
         )
 
-    share(group, pair)
-
     @pl.when(group > 0)
     def share_far():
         share(group, far, groups)
 
+    share(group, pair)
     eye = lax.broadcasted_iota(jnp.int32, (slots, slots), 0) == lax.broadcasted_iota(
         jnp.int32, (slots, slots), 1
     )
@@ -239,49 +238,81 @@
             swap_copy(j).start()
             sums[:, cols] = rows[:TOK_DEV]
 
-    for k in range(groups):
-        if k in (1, 2):
-            wait_shared(sources[k])
-
-            @pl.when(group == 1 if k == 1 else group < last)
-            def forward():
-                share(sources[k], far if k == 1 else pair)
-
-        if k == last:
-
-            @pl.when(group != last - 1)
-            def wait_last():
-                wait_shared(sources[k])
-
-        if k:
-            for m in column_steps:
-                place_copy(k, m).start()
-        if k == 1:
-            pair_places[column] = meta[pl.ds(pair_base, 2), 1]
-        elif k > 1:
-            places[k - 2, column] = meta[sources[k], 1]
+    def compute(k):
         factor = jnp.sum(jnp.where(eye, meta[sources[k], 0, :, :slots], 0.0), axis=1, keepdims=True)
-        batch = 1
-        for j in range((half if k < 2 else width) // piece):
+        def product(j):
             if k == 0 or k == 2 and j >= half // piece:
                 weight_copy(j).wait()
             cols = slice(j * piece, (j + 1) * piece)
-            product = jnp.dot(rows_in[sources[k]], weight[:, cols], preferred_element_type=jnp.float32)
-            scaled = product * factor
+            return jnp.dot(rows_in[sources[k]], weight[:, cols], preferred_element_type=jnp.float32)
+
+        steps = (half if k < 2 else width) // piece
+        ahead = product(0)
+        for j in range(steps):
+            scaled = ahead * factor
+            if j + 1 < steps:
+                ahead = product(j + 1)
+            cols = slice(j * piece, (j + 1) * piece)
             for q in range(columns):
                 rows_out(k)[q, :, cols] = scaled[q * send:(q + 1) * send].astype(jnp.bfloat16)
-            if (j + 1) % batch == 0:
-                for m in column_steps:
-                    row_copy(k, m, j + 1 - batch, batch).start()
+            for m in column_steps:
+                row_copy(k, m, j, 1).start()
         rows_at(k)[column] = rows_out(k)[column]
-        if k == 2:
-
-            @pl.when(group == last - 1)
-            def forward_last():
-                wait_shared(sources[last])
-                share(sources[last], pair)
-
-            early_sums()
+
+    def take_pair():
+        wait_shared(sources[1])
+
+        @pl.when(group == 1)
+        def forward_pair():
+            share(sources[1], far)
+
+        for m in column_steps:
+            place_copy(1, m).start()
+        pair_places[column] = meta[pl.ds(pair_base, 2), 1]
+        compute(1)
+
+    def take_third():
+        wait_shared(sources[2])
+
+        @pl.when(group < last)
+        def forward_third():
+            share(sources[2], pair)
+
+        for m in column_steps:
+            place_copy(2, m).start()
+        places[0, column] = meta[sources[2], 1]
+        compute(2)
+
+    compute(0)
+
+    @pl.when(group != last - 1)
+    def pair_first():
+        take_pair()
+        take_third()
+
+    @pl.when(group == last - 1)
+    def third_first():
+        take_third()
+        wait_shared(sources[last])
+        share(sources[last], pair)
+        take_pair()
+
+    @pl.when(lax.rem(group, 2) == 1)
+    def early_first():
+        early_sums()
+
+    @pl.when(group != last - 1)
+    def wait_last():
+        wait_shared(sources[last])
+
+    for m in column_steps:
+        place_copy(last, m).start()
+    places[last - 2, column] = meta[sources[last], 1]
+    compute(last)
+
+    @pl.when(lax.rem(group, 2) == 0)
+    def early_after():
+        early_sums()
 
     tables = []
     for k in range(2, groups):

time: 20 us -> 19.1 us (0.955)
  Pallas kernels: 19.8 us -> 18.9 us
    pallas_call x1, Pallas kernels: 18.9 us -> 18 us  [kernel_body(): pl.pallas_call(functools.partial(kernel, groups, columns, send, PIECE), o...]
where the time goes in v3:
time: 19.1 us; the launch traced here: 18.9 us
  Pallas kernels  18.9 us (99%)
    pallas_call x1, Pallas kernels, kernel_body(): pl.pallas_call(functools.partial(kernel, groups, columns, send, PIECE), o...  18 us
    pallas_call x1, Pallas kernels, kernel_body(): pl.pallas_call(functools.partial(finish, PIECE), out_shape=jax.ShapeDtype...  0.89 us

profile of v3, /device:TPU:0, one launch (start us, length us, event | category | flops | bytes accessed | tf_op | source)
XLA Modules:
  0.0 18.9 jit_solution(1064844869050971412)
XLA Ops:
  0.0 18.0 %shard_map.64 = (f32[32,4096]{1,0:T(8,128)S(1)}, bf16[8,4,4096]{2,1,0:T(4,128)(2,1)S(1)}, bf16[32,32]{1,0:T(8,128)(2,1)S(1)}) custom-call(bf16[1,1,32,1024]{3,2,1,0:T(8,128)(2,1)} %hidden_ref.1, bf16[1,1024,4096]{2,1,0:T(8,128)(2,1)} %weight_ref.1, f32[1,1,32]{2,1,0:T(1,128)} %gate_ref.1, s32[1,1,32]{2,1,0:T(1,128)} %owner_ref.1, s32[1,1,32]{2,1,0:T(1,128)} %row_ref.1, ...), custom_call_target="tpu_custom_call" | custom-call | tf_op jit(solution)/shard_map/pallas_call | solution.py:393
  18.0 0.9 %shard_map.65 = bf16[32,4096]{1,0:T(8,128)(2,1)} custom-call(f32[32,4096]{1,0:T(8,128)S(1)} %get-tuple-element.8.sums, bf16[8,4,4096]{2,1,0:T(4,128)(2,1)S(1)} %get-tuple-element.9.last_rows, bf16[32,32]{1,0:T(8,128)(2,1)S(1)} %get-tuple-element.10.last_table), custom_call_target="tpu_custom_call" | custom-call | tf_op jit(solution)/shard_map/pallas_call | solution.py:427

commit v4 on v3

--- a/solution.py
+++ b/solution.py
@@ -11,6 +11,7 @@
 LANES = 128
 PIECE = 1024
 PLANES = 4
+COLUMNS = 8
 VMEM_ROOM = 48 * 1024 * 1024
 MESH = pl.DeviceIdType.MESH
 
@@ -61,7 +62,7 @@
     sums, last_rows, last_table,
     gate, owner, row, count, weight, rows_in, meta,
     out_early, out_late, in_early, in_late, pair_places, places, swap_out, swap_in,
-    load_sem, weight_sem, hid_send, hid_recv, meta_send, meta_recv,
+    load_sem, weight_sem, corner, hid_send, hid_recv, meta_send, meta_recv,
     row_send, row_recv, place_send, place_recv, swap_send, swap_recv,
 ):
     group, column = lax.axis_index("grp"), lax.axis_index("ep")
@@ -74,7 +75,7 @@
     far, far_pair = last - group, last - pair
     end = group == last
     sources = [group, pair, jnp.where(end, far_pair, far), jnp.where(end, far, far_pair)]
-    column_steps = sorted(range(1, columns), key=lambda k: (k % 2, -k))
+    column_steps = [6, 7, 4, 5, 2, 3, 1]
 
     def weight_copy(j):
         return pltpu.make_async_copy(
@@ -94,7 +95,8 @@
         load.start()
 
     barrier = pltpu.get_barrier_semaphore()
-    for k in column_steps:
+    near_steps = [k for k in column_steps if k // 2 in (0, 1, 2)]
+    for k in near_steps:
         pl.semaphore_signal(
             barrier, inc=1, device_id=(group, partner(column, columns, k)[0]), device_id_type=MESH
         )
@@ -117,7 +119,7 @@
     meta[group, 0, :, :slots] = scale
     meta[group, 1, :, :slots] = (owner[...] * TOK_DEV + row[...]).astype(jnp.float32)
 
-    pl.semaphore_wait(barrier, columns + jnp.where(group > 0, 1, 0))
+    pl.semaphore_wait(barrier, len(near_steps) + 1 + jnp.where(group > 0, 1, 0))
 
     def share_copies(at, to, slot=None):
         slot = at if slot is None else slot
@@ -195,6 +197,9 @@
         share(group, far, groups)
 
     share(group, pair)
+    pl.semaphore_signal(
+        corner, inc=1, device_id=(group, partner(column, columns, 2)[0]), device_id_type=MESH
+    )
     eye = lax.broadcasted_iota(jnp.int32, (slots, slots), 0) == lax.broadcasted_iota(
         jnp.int32, (slots, slots), 1
     )
@@ -252,6 +257,8 @@
             scaled = ahead * factor
             if j + 1 < steps:
                 ahead = product(j + 1)
+            if k == 0 and j == 0:
+                pl.semaphore_wait(corner, 1)
             cols = slice(j * piece, (j + 1) * piece)
             for q in range(columns):
                 rows_out(k)[q, :, cols] = scaled[q * send:(q + 1) * send].astype(jnp.bfloat16)
@@ -415,7 +422,7 @@
             pltpu.VMEM((groups - 2, columns, 1, lanes), jnp.float32),
             pltpu.VMEM((TOK_DEV, width // 2), jnp.bfloat16),
             pltpu.VMEM((TOK_DEV, width // 2), jnp.bfloat16),
-            dma((5,)), dma((pieces,)),
+            dma((5,)), dma((pieces,)), pltpu.SemaphoreType.REGULAR,
             dma((groups + 1,)), dma((groups,)), dma((groups + 1,)), dma((groups,)),
             dma((groups,)), dma((groups,)), dma((groups - 1,)), dma((groups - 1,)),
             dma((halves,)), dma((halves,)),
@@ -439,7 +446,7 @@
     slots, depth = hidden.shape[2:]
     width = down_weight.shape[2]
     held = 2 * (depth * width + groups * slots * (depth + 2 * width))
-    even = groups == PLANES and columns > 1 and width % (2 * PIECE) == 0
+    even = groups == PLANES and columns == COLUMNS and width % (2 * PIECE) == 0
     fits = held <= VMEM_ROOM and even
     chosen = kernel_body if fits else exchange_body
     return chosen(hidden, down_weight, *slot_data)

time: 19.1 us -> 19.1 us (level)
  no operation moved by 1% of the time
where the time goes in v4:
time: 19.1 us; the launch traced here: 18.9 us
  Pallas kernels  18.9 us (99%)
    pallas_call x1, Pallas kernels, kernel_body(): pl.pallas_call(functools.partial(kernel, groups, columns, send, PIECE), o...  18 us
    pallas_call x1, Pallas kernels, kernel_body(): pl.pallas_call(functools.partial(finish, PIECE), out_shape=jax.ShapeDtype...  0.89 us

profile of v4, /device:TPU:0, one launch (start us, length us, event | category | flops | bytes accessed | tf_op | source)
XLA Modules:
  0.0 18.9 jit_solution(5730749120137819040)
XLA Ops:
  0.0 18.0 %shard_map.64 = (f32[32,4096]{1,0:T(8,128)S(1)}, bf16[8,4,4096]{2,1,0:T(4,128)(2,1)S(1)}, bf16[32,32]{1,0:T(8,128)(2,1)S(1)}) custom-call(bf16[1,1,32,1024]{3,2,1,0:T(8,128)(2,1)} %hidden_ref.1, bf16[1,1024,4096]{2,1,0:T(8,128)(2,1)} %weight_ref.1, f32[1,1,32]{2,1,0:T(1,128)} %gate_ref.1, s32[1,1,32]{2,1,0:T(1,128)} %owner_ref.1, s32[1,1,32]{2,1,0:T(1,128)} %row_ref.1, ...), custom_call_target="tpu_custom_call" | custom-call | tf_op jit(solution)/shard_map/pallas_call | solution.py:400
  18.0 0.9 %shard_map.65 = bf16[32,4096]{1,0:T(8,128)(2,1)} custom-call(f32[32,4096]{1,0:T(8,128)S(1)} %get-tuple-element.8.sums, bf16[8,4,4096]{2,1,0:T(4,128)(2,1)S(1)} %get-tuple-element.9.last_rows, bf16[32,32]{1,0:T(8,128)(2,1)S(1)} %get-tuple-element.10.last_table), custom_call_target="tpu_custom_call" | custom-call | tf_op jit(solution)/shard_map/pallas_call | solution.py:434
